TPU v7x, 32 devices: a whole 2x2x4 slice. The times are simulated.
32 devices in a mesh: dp: 8 (over z, y), grp: 4 (over x, core).
Axes of the slice: x: 2, y: 2, z: 4, core: 2. Of those that a mesh axis runs over, the one named last changes fastest.
Arguments:
- quot_ids: int32 [4096, 2], P(('dp', 'grp')), may hold values from 0 to 127
- rem_ids: int32 [4096, 2], P(('dp', 'grp')), may hold values from 0 to 16383, as said below
- labels: int32 [4096], P(('dp', 'grp')), may hold values 0 or 1
- quot_table: bfloat16 [2, 128, 512], replicated, may hold values from -6 to 6
- rem_table: bfloat16 [2, 16384, 512], P(None, 'grp'), may hold values from -6 to 6
- w1: bfloat16 [1024, 512], replicated, may hold values from -0.1875 to 0.1875
- b1: float32 [512], replicated, may hold values from -3 to 3
- w2: bfloat16 [512], replicated, may hold values from -0.5 to 0.5
- b2: float32 [1], replicated, may hold values from -3 to 3
Outputs:
- losses: float32 [4096], P(('dp', 'grp'))
- grad_rem: float32 [2, 16384, 512], P(None, 'grp', 'dp')
- grad_quot: float32 [2, 128, 512], replicated
- grad_w1: float32 [1024, 512], replicated
- grad_b1: float32 [512], replicated
- grad_w2: float32 [512], replicated
- grad_b2: float32 [1], replicated
Inputs may be any that keep to these rules, and one draw needn't show every extreme that they name: `rem_ids`: in each aligned block of 128 samples and each feature, at most 64 remainder indices r share the same r // 4096, and exactly 64 do for some value of r // 4096.
All inputs are finite; a program needn't handle non-finite values. No bound on the sum of `labels` on one device may be relied on, other than what follows from the above.
Results may differ from a plain program's by a relative error of at most 0.0051.
Values may be sent and summed in bfloat16 or wider, within the bound.
No kernel may reach another device: no remote copies, remote signals or barrier semaphores. Data moves between devices by JAX's collectives and lax.ppermute only.
A program may use at most 128 MiB of HBM per device.

v0:
```python
import jax
import jax.numpy as jnp
from jax import lax
from jax.sharding import PartitionSpec as P


def scatter_rows(shard_grad, positions, values):
    for feature in range(shard_grad.shape[0]):
        shard_grad = shard_grad.at[feature, positions[:, feature]].add(
            values[:, feature].astype(jnp.float32), mode="drop"
        )
    return shard_grad


def pick_rows(rem_table, wanted, filled):
    pieces = []
    for feature in range(rem_table.shape[0]):
        picked = jnp.take(rem_table[feature], wanted[:, feature], axis=0)
        pieces.append(jnp.where(filled[:, feature : feature + 1], picked, jnp.zeros_like(picked)))
    return jnp.concatenate(pieces, axis=1)


def on_device(quot_ids, rem_ids, labels, quot_table, rem_table, w1, b1, w2, b2):
    features = rem_ids.shape[1]
    shard_rows = rem_table.shape[1]
    model_width = rem_table.shape[2]
    table_rows = quot_table.shape[1]
    owner_index = lax.axis_index("grp")
    gathered_ids = lax.all_gather(rem_ids, "grp", axis=0, tiled=True)
    local_rows = gathered_ids - owner_index * shard_rows
    inside = (local_rows >= 0) & (local_rows < shard_rows)
    safe_rows = jnp.clip(local_rows, 0, shard_rows - 1)
    partial_value = pick_rows(rem_table, safe_rows, inside).astype(jnp.float32)
    rem_rows = lax.psum_scatter(
        partial_value.astype(jnp.bfloat16), "grp", scatter_dimension=0, tiled=True
    )
    quot_parts = []
    onehots = []
    for feature in range(features):
        onehot = (
            quot_ids[:, feature][:, None] == jnp.arange(table_rows, dtype=jnp.int32)[None, :]
        ).astype(jnp.bfloat16)
        onehots.append(onehot)
        quot_parts.append(jnp.dot(onehot, quot_table[feature], preferred_element_type=jnp.float32))
    quot_rows = jnp.concatenate(quot_parts, axis=1)
    rem_float = rem_rows.astype(jnp.float32)
    joined = (quot_rows * rem_float).astype(jnp.bfloat16)
    preact = jnp.dot(joined, w1, preferred_element_type=jnp.float32) + b1
    hidden = jax.nn.silu(preact).astype(jnp.bfloat16)
    logits = jnp.dot(hidden, w2, preferred_element_type=jnp.float32) + b2[0]
    target = labels.astype(jnp.float32)
    losses = jax.nn.softplus(logits) - target * logits
    dlogits = jax.nn.sigmoid(logits) - target
    grad_b2 = jnp.sum(dlogits)[None]
    grad_w2 = jnp.dot(dlogits, hidden.astype(jnp.float32), precision=lax.Precision.HIGHEST)
    sigmoid_pre = jax.nn.sigmoid(preact)
    slopes = sigmoid_pre * (1.0 + preact * (1.0 - sigmoid_pre))
    dpreact = dlogits[:, None] * w2.astype(jnp.float32)[None, :] * slopes
    grad_b1 = jnp.sum(dpreact, axis=0)
    rounded = dpreact.astype(jnp.bfloat16)
    grad_w1 = jnp.dot(joined.T, rounded, preferred_element_type=jnp.float32)
    djoined = jnp.dot(rounded, w1.T, preferred_element_type=jnp.float32)
    rem_grads = (djoined * quot_rows).astype(jnp.bfloat16)
    quot_grads = djoined * rem_float
    quot_list = []
    for feature in range(features):
        quot_list.append(
            jnp.dot(
                onehots[feature].astype(jnp.float32).T,
                quot_grads[:, feature * model_width : (feature + 1) * model_width],
                precision=lax.Precision.HIGHEST,
            )
        )
    grad_quot = jnp.stack(quot_list, axis=0)
    grad_w1, grad_b1, grad_w2, grad_b2, grad_quot = lax.psum(
        (grad_w1, grad_b1, grad_w2, grad_b2, grad_quot), ("dp", "grp")
    )
    group_rows = lax.all_gather(rem_grads, "grp", axis=0, tiled=True)
    group_rows = group_rows.reshape(group_rows.shape[0], features, model_width)
    positions = jnp.where(inside, local_rows, shard_rows)
    received = lax.all_to_all(group_rows, "dp", split_axis=2, concat_axis=0, tiled=True)
    all_positions = lax.all_gather(positions, "dp", axis=0, tiled=True)
    shard_grad = jnp.zeros((features, shard_rows, received.shape[2]), jnp.float32)
    grad_rem = scatter_rows(shard_grad, all_positions, received)
    return (losses, grad_rem, grad_quot, grad_w1, grad_b1, grad_w2, grad_b2)


def solution(mesh):
    placed = (
        P(("dp", "grp"), None),
        P(("dp", "grp"), None),
        P(("dp", "grp")),
        P(),
        P(None, "grp", None),
        P(),
        P(),
        P(),
        P(),
    )
    return jax.shard_map(
        on_device,
        mesh=mesh,
        in_specs=placed,
        out_specs=(P(("dp", "grp")), P(None, "grp", "dp"), P(), P(), P(), P(), P()),
        check_vma=False,
    )
```

profile of v0, /device:TPU:0, one launch (start us, length us, event | category | flops | bytes accessed | tf_op | source)
XLA Modules:
  0.0 262.6 jit_solution(8166397708621926012)
XLA Ops:
  7.2 0.0 copy-start
  7.2 0.0 reduce-scatter.2.cloned.1.call-start
  7.2 6.4 %all_gather.9 = s32[512,2]{0,1:T(2,128)S(1)} all-gather(s32[128,2]{0,1:T(2,128)} %param.12), channel_id=1, replica_groups=mesh['dp'=8,'grp'=4] {'grp'}, dimensions={0}, use_global_device_ids=true | all-gather | bytes 5120 | tf_op jit(solution)/shard_map/all_gather | solution.py:29
  13.7 5.7 %slice_bitcast_fusion.1 = (bf16[4096,512]{1,0:T(8,128)(2,1)}, bf16[4096,512]{1,0:T(8,128)(2,1)}) fusion(bf16[2,4096,512]{2,1,0:T(8,128)(2,1)} %param.15), kind=kLoop, calls=%fused_computation.5 | loop fusion | bytes 16777216 | tf_op jit(solution)/shard_map/squeeze | solution.py:18
  19.5 4.7 %gather_fusion.1 = bf16[512,512]{1,0:T(8,128)(2,1)S(1)} fusion(bf16[4096,512]{1,0:T(8,128)(2,1)} %get-tuple-element.43, s32[1024]{0:T(1024)S(1)} %pad_clamp_fusion), kind=kCustom, calls=%fused_computation.1.clone | custom fusion | bytes 1050624 | tf_op jit(solution)/shard_map/jit(_take)/gather | solution.py:18
  24.2 0.0 copy-start.6
  24.3 0.0 copy-start.7
  24.3 0.0 copy-start.1
  24.3 4.8 %gather_fusion = bf16[512,512]{1,0:T(8,128)(2,1)S(1)} fusion(bf16[4096,512]{1,0:T(8,128)(2,1)} %get-tuple-element.42, s32[1024]{0:T(1024)S(1)} %pad_clamp_fusion.1), kind=kCustom, calls=%fused_computation.clone | custom fusion | bytes 1050624 | tf_op jit(solution)/shard_map/jit(_take)/gather | solution.py:18
  29.0 0.0 copy-start.11
  29.1 0.0 copy-start.8
  29.1 0.6 select_select_fusion
  29.6 1.1 pad_maximum_fusion
  30.7 0.0 reduce-scatter.2.cloned.1.call-update
  30.8 0.0 all-gather.2.cloned.1.call-start
  30.8 0.0 copy-done.6
  30.8 0.0 copy-start.2
  31.5 0.0 copy-done.7
  31.5 0.0 copy-start.5
  31.5 0.0 copy-start.4
  31.6 0.0 copy-done.1
  31.6 0.2 fusion.8
  31.8 0.3 copy-done.5
  32.0 0.2 fusion.10
  32.3 25.1 %reduce-scatter.2.cloned.1.call-done = bf16[128,1024]{1,0:T(8,128)(2,1)} async-done(((bf16[512,1024]{1,0:T(8,128)(2,1)}), bf16[128,1024]{1,0:T(8,128)(2,1)}) %reduce-scatter.2.cloned.1.call-update) | async-done | bytes 262160 | tf_op jit(solution)/shard_map/reduce_scatter | solution.py:34
  57.4 0.0 copy-done
  57.4 0.0 copy-done.11
  57.4 1.3 multiply_convert_fusion.1
  58.7 0.0 copy-done.8
  58.7 1.3 fusion.30
  60.0 0.0 copy-done.4
  60.0 2.2 convert_multiply_fusion
  62.2 0.0 all-gather.2.cloned.1.call-update
  62.2 32.3 %all_gather.10 = s32[4096,2]{0,1:T(2,128)} all-gather(s32[512,2]{0,1:T(2,128)S(1)} %get-tuple-element.50), channel_id=1, replica_groups=mesh['dp'=8,'grp'=4] {'dp'}, dimensions={0}, use_global_device_ids=true | all-gather | bytes 36864 | tf_op jit(solution)/shard_map/all_gather | solution.py:82
  94.5 0.0 copy-done.3
  94.5 0.0 all-gather.2.cloned.1.call-done
  94.5 1.8 reshape.29
  96.4 3.8 %copy.25 = bf16[512,2,512]{0,1,2:T(2,128)(2,1)} copy(bf16[512,2,512]{2,1,0:T(2,128)(2,1)S(1)} %reshape.29) | data formatting | bytes 2097152 | tf_op jit(solution)/shard_map/reshape | solution.py:79
  100.1 5.4 %all-to-all-start = ((bf16[512,2,512]{0,1,2:T(2,128)(2,1)}), bf16[512,2,512]{0,1,2:T(2,128)(2,1)S(1)}, u32[]{:S(2)}, u32[]{:S(2)}) async-start(bf16[512,2,512]{0,1,2:T(2,128)(2,1)} %copy.25), calls=%async_computation.1 | async-start | bytes 2097152 | tf_op jit(solution)/shard_map/all_to_all | solution.py:81
  105.5 0.0 all-reduce.6.cloned.1.call-start
  105.6 0.9 compare_select_fusion.1
  106.4 0.1 fusion.19
  106.6 0.2 and_reduce_fusion
  106.8 0.6 broadcast_select_fusion
  107.4 1.0 convolution_bitcast_fusion
  108.5 1.0 convolution_bitcast_fusion.1
  109.5 0.8 pad_maximum_fusion.2
  110.3 2.8 %fusion.14 = f32[1024,512]{1,0:T(8,128)} fusion(bf16[128,1024]{1,0:T(8,128)(2,1)} %reduce-scatter.2.cloned.1.call-done, f32[128,512]{1,0:T(8,128)S(1)} %fusion.8, f32[128,512]{1,0:T(8,128)S(1)} %fusion.10, f32[128,512]{1,0:T(8,128)S(1)} %get-tuple-element.58, f32[512]{0:T(512)} %copy-done.2, f32[128]{0:T(128)} %copy-done.3), kind=kOutput, calls=%fused_computation.39 | convolution fusion | flops 135397376 | bytes 3148288 | tf_op jit(solution)/shard_map/dot_general | solution.py:61
  113.1 0.0 all-reduce.6.cloned.1.call-update
  113.2 0.8 fusion.29
  114.0 0.8 fusion.25
  114.8 40.5 %all-reduce.2 = (f32[512]{0:T(512)}, f32[512]{0:T(512)}, f32[1]{0:T(128)}) all-reduce(f32[512]{0:T(512)S(1)} %fusion.29, f32[512]{0:T(512)S(1)} %bitcast.59, f32[1]{0:T(128)} %bitcast.19), channel_id=1, replica_groups=mesh['dp'=8,'grp'=4] {'dp','grp'}, use_global_device_ids=true, to_apply=%region_6.8 | all-reduce | flops 1025 | bytes 8200 | tf_op jit(solution)/shard_map/psum | solution.py:75
  155.3 0.0 all-to-all-done
  155.3 0.2 copy.26
  155.5 0.1 copy.34
  155.6 1.2 fusion.4
  156.8 1.9 copy.28
  158.7 1.8 copy.29
  160.5 24.8 %scatter_custom_fusion = f32[8192,64]{1,0:T(8,128)} fusion(s32[4096]{0:T(1024)} %get-tuple-element.62, f32[4096,64]{1,0:T(8,128)} %copy.28, f32[]{:T(128)} %constant.3.clone.1), kind=kCustom, calls=%fused_computation.6 | custom fusion | flops 262144 | bytes 2097664
  185.4 24.2 %scatter_fusion = f32[8192,64]{1,0:T(8,128)} fusion(f32[8192,64]{1,0:T(8,128)} %scatter_custom_fusion, s32[4096]{0:T(1024)S(1)} %get-tuple-element.61, f32[4096,64]{1,0:T(8,128)S(1)} %copy.29), kind=kCustom, calls=%fused_computation.3 | custom fusion | flops 262144 | bytes 3162112
  209.6 3.8 %copy.31 = f32[2,4096,64]{1,2,0:T(8,128)} copy(f32[2,4096,64]{2,1,0:T(8,128)} %bitcast.52) | data formatting | bytes 4194304
  213.4 37.7 %all-reduce.6.cloned.1.call-done = (f32[2,128,512]{2,1,0:T(8,128)}, f32[1024,512]{1,0:T(8,128)}) async-done(((f32[2,128,512]{2,1,0:T(8,128)}, f32[1024,512]{1,0:T(8,128)}), (f32[2,128,512]{2,1,0:T(8,128)}, f32[1024,512]{1,0:T(8,128)})) %all-reduce.6.cloned.1.call-update) | async-done | bytes 2621456 | tf_op jit(solution)/shard_map/psum | solution.py:75
  251.1 1.9 copy.39
  253.0 3.1 %copy.40 = f32[1024,512]{1,0:T(8,128)} copy(f32[1024,512]{1,0:T(8,128)} %get-tuple-element.66) | data formatting | bytes 4194304
  (19 shorter events, 0.1 us)
Async XLA Ops:
  7.2 50.3 %copy-start = (bf16[1024,512]{1,0:T(8,128)(2,1)S(1)}, bf16[1024,512]{1,0:T(8,128)(2,1)}, u32[]{:S(2)}) copy-start(bf16[1024,512]{1,0:T(8,128)(2,1)} %param.16) | copy-start | bytes 3145732
  7.2 50.2 %reduce-scatter.2.cloned.1.call-start = ((), (), s32[]{:S(2)}) async-start(), calls=%async_computation.2 | async-start | bytes 1310720 | tf_op jit(solution)/shard_map/reduce_scatter | solution.py:34
  24.2 6.6 %copy-start.6 = (bf16[512]{0:T(512)(128)(2,1)S(1)}, bf16[512]{0:T(512)(128)(2,1)}, u32[]{:S(2)}) copy-start(bf16[512]{0:T(512)(128)(2,1)} %param.18) | copy-start | bytes 3076
  24.3 7.3 %copy-start.7 = (s32[128,2]{0,1:T(2,128)S(1)}, s32[128,2]{0,1:T(2,128)}, u32[]{:S(2)}) copy-start(s32[128,2]{0,1:T(2,128)} %param.11) | copy-start | bytes 3076
  24.3 7.3 %copy-start.1 = (bf16[2,128,512]{2,1,0:T(8,128)(2,1)S(1)}, bf16[2,128,512]{2,1,0:T(8,128)(2,1)}, u32[]{:S(2)}) copy-start(bf16[2,128,512]{2,1,0:T(8,128)(2,1)} %param.14) | copy-start | bytes 786436
  29.0 28.4 %copy-start.11 = (f32[512]{0:T(512)S(1)}, f32[512]{0:T(512)}, u32[]{:S(2)}) copy-start(f32[512]{0:T(512)} %param.17) | copy-start | bytes 6148
  29.1 29.7 %copy-start.8 = (s32[128]{0:T(128)S(1)}, s32[128]{0:T(128)}, u32[]{:S(2)}) copy-start(s32[128]{0:T(128)} %param.13) | copy-start | bytes 1540
  30.8 63.7 %all-gather.2.cloned.1.call-start = ((), (), s32[]{:S(2)}) async-start(), calls=%async_computation.3 | async-start | bytes 1310720 | tf_op jit(solution)/shard_map/all_gather | solution.py:78
  30.8 63.6 %copy-start.2 = (f32[512]{0:T(512)}, f32[512]{0:T(512)S(1)}, u32[]{:S(2)}) copy-start(f32[512]{0:T(512)S(1)} %convert_element_type.44) | copy-start | bytes 6148
  31.5 0.5 copy-start.5
  31.5 28.5 %copy-start.4 = (s32[128]{0:T(128)}, s32[128]{0:T(128)S(1)}, u32[]{:S(2)}) copy-start(s32[128]{0:T(128)S(1)} %get-tuple-element.55) | copy-start | bytes 1540
  60.0 34.5 %copy-start.3 = (f32[128]{0:T(128)}, f32[128]{0:T(128)S(1)}, u32[]{:S(2)}) copy-start(f32[128]{0:T(128)S(1)} %get-tuple-element.41) | copy-start | bytes 1540
  60.0 46.4 %copy-start.9 = (s32[2]{0:T(128)S(1)}, s32[2]{0:T(128)}, u32[]{:S(2)}) copy-start(s32[2]{0:T(128)} %constant.13) | copy-start | bytes 28
  60.0 46.6 %copy-start.10 = (s32[2]{0:T(128)S(1)}, s32[2]{0:T(128)}, u32[]{:S(2)}) copy-start(s32[2]{0:T(128)} %constant.28) | copy-start | bytes 28
  100.1 55.2 %all-to-all-start = ((bf16[512,2,512]{0,1,2:T(2,128)(2,1)}), bf16[512,2,512]{0,1,2:T(2,128)(2,1)S(1)}, u32[]{:S(2)}, u32[]{:S(2)}) async-start(bf16[512,2,512]{0,1,2:T(2,128)(2,1)} %copy.25), calls=%async_computation.1 | async-start | bytes 2097152 | tf_op jit(solution)/shard_map/all_to_all | solution.py:81
  105.5 145.6 %all-reduce.6.cloned.1.call-start = ((), (), s32[]{:S(2)}) async-start(), calls=%async_computation.4 | async-start | bytes 5242880 | tf_op jit(solution)/shard_map/psum | solution.py:75
Sparse Core Ops, SparseCore 0:
  30.9 26.4 reduce-scatter.1
  62.3 16.6 all-gather.1
  113.3 137.7 all-reduce.5
where the time goes:
time: 263 us
  blocking collectives  79.2 us (30%)
  waiting for transfers between devices  62.9 us (24%)
  other arithmetic  55.4 us (21%)
  local copies, waits for them, and re-layouts  33.9 us (13%)
  between operations  14.7 us (6%)
  matrix products  10.9 us (4%)
  starting transfers between devices  5.49 us (2%)
    unnamed x5, other arithmetic  50 us
    psum x1, blocking collectives, on_device(): lax.psum((grad_w1, grad_b1, grad_w2, grad_b2, grad_quot), ('dp', 'grp'))  40.5 us
    psum x1, waiting for transfers between devices, on_device(): lax.psum((grad_w1, grad_b1, grad_w2, grad_b2, grad_quot), ('dp', 'grp'))  37.7 us
    all_gather x1, blocking collectives, on_device(): all_positions = lax.all_gather(positions, 'dp', axis=0, tiled=True)  32.3 us
    reduce_scatter x1, waiting for transfers between devices, on_device(): lax.psum_scatter(partial_value.astype(jnp.bfloat16), 'grp', scatter_dimen...  25.1 us
    gather x2, local copies, waits for them, and re-layouts, pick_rows(): picked = jnp.take(rem_table[feature], wanted[:, feature], axis=0)  9.47 us
    unnamed x28, local copies, waits for them, and re-layouts  9.05 us
    all_gather x1, blocking collectives, on_device(): gathered_ids = lax.all_gather(rem_ids, 'grp', axis=0, tiled=True)  6.42 us
  transfers between devices with their start and end apart: 4, of which 2 were waited for; matrix products, arithmetic and copies ran while one was open for 26% of the time, Pallas kernels for 0%

commit v1 on v0

--- a/solution.py
+++ b/solution.py
@@ -73,7 +73,7 @@
         )
     grad_quot = jnp.stack(quot_list, axis=0)
     grad_w1, grad_b1, grad_w2, grad_b2, grad_quot = lax.psum(
-        (grad_w1, grad_b1, grad_w2, grad_b2, grad_quot), ("dp", "grp")
+        lax.psum((grad_w1, grad_b1, grad_w2, grad_b2, grad_quot), "grp"), "dp"
     )
     group_rows = lax.all_gather(rem_grads, "grp", axis=0, tiled=True)
     group_rows = group_rows.reshape(group_rows.shape[0], features, model_width)

time: 263 us -> 273 us (1.038)
  waiting for transfers between devices: 62.9 us -> 75.3 us
  blocking collectives: 79.2 us -> 83.1 us
  matrix products: 10.9 us -> 7.06 us
    all_gather x1, blocking collectives: 32.3 us -> 46.2 us  [on_device(): all_positions = lax.all_gather(positions, 'dp', axis=0, tiled=True)]
    all_gather x1, waiting for transfers between devices: 0.02 us -> 13.3 us  [on_device(): group_rows = lax.all_gather(rem_grads, 'grp', axis=0, tiled=True)]
    psum x1 -> x2, blocking collectives: 40.5 us -> 30.5 us  [the longest x1 23.9 us: on_device(): lax.psum(lax.psum((grad_w1, grad_b1, grad_w2, grad_b2, grad_quot), 'grp')...]
    psum x1 -> x2, waiting for transfers between devices: 37.7 us -> 36.4 us  [the longest x1 31.1 us: on_device(): lax.psum(lax.psum((grad_w1, grad_b1, grad_w2, grad_b2, grad_quot), 'grp')...]
    unnamed x28 -> x22, local copies, waits for them, and re-layouts: 9.05 us -> 8.86 us
  transfers between devices with their start and end apart: 4 -> 5, of which waited for: 2 -> 4; matrix products, arithmetic and copies ran while one was open for 26% -> 25% of each run, Pallas kernels for 0% -> 0%
where the time goes in v1:
time: 273 us
  blocking collectives  83.1 us (30%)
  waiting for transfers between devices  75.3 us (28%)
  other arithmetic  53.3 us (20%)
  local copies, waits for them, and re-layouts  33.7 us (12%)
  between operations  14.7 us (5%)
  matrix products  7.06 us (3%)
  starting transfers between devices  5.81 us (2%)
    unnamed x5, other arithmetic  49.4 us
    all_gather x1, blocking collectives, on_device(): all_positions = lax.all_gather(positions, 'dp', axis=0, tiled=True)  46.2 us
    psum x1, waiting for transfers between devices, on_device(): lax.psum(lax.psum((grad_w1, grad_b1, grad_w2, grad_b2, grad_quot), 'grp')...  31.1 us
    reduce_scatter x1, waiting for transfers between devices, on_device(): lax.psum_scatter(partial_value.astype(jnp.bfloat16), 'grp', scatter_dimen...  25.4 us
    psum x1, blocking collectives, on_device(): lax.psum(lax.psum((grad_w1, grad_b1, grad_w2, grad_b2, grad_quot), 'grp')...  23.9 us
    all_gather x1, waiting for transfers between devices, on_device(): group_rows = lax.all_gather(rem_grads, 'grp', axis=0, tiled=True)  13.3 us
    gather x2, local copies, waits for them, and re-layouts, pick_rows(): picked = jnp.take(rem_table[feature], wanted[:, feature], axis=0)  9.42 us
    unnamed x22, local copies, waits for them, and re-layouts  8.86 us
  transfers between devices with their start and end apart: 5, of which 4 were waited for; matrix products, arithmetic and copies ran while one was open for 25% of the time, Pallas kernels for 0%

profile of v1, /device:TPU:0, one launch (start us, length us, event | category | flops | bytes accessed | tf_op | source)
XLA Modules:
  0.0 272.9 jit_solution(6802329701022157155)
XLA Ops:
  7.2 0.0 copy-start
  7.2 0.0 reduce-scatter.2.cloned.1.call-start
  7.2 6.4 %all_gather.9 = s32[512,2]{0,1:T(2,128)S(1)} all-gather(s32[128,2]{0,1:T(2,128)} %param.12), channel_id=1, replica_groups=mesh['dp'=8,'grp'=4] {'grp'}, dimensions={0}, use_global_device_ids=true | all-gather | bytes 5120 | tf_op jit(solution)/shard_map/all_gather | solution.py:29
  13.7 5.7 %slice_bitcast_fusion.1 = (bf16[4096,512]{1,0:T(8,128)(2,1)}, bf16[4096,512]{1,0:T(8,128)(2,1)}) fusion(bf16[2,4096,512]{2,1,0:T(8,128)(2,1)} %param.15), kind=kLoop, calls=%fused_computation.5 | loop fusion | bytes 16777216 | tf_op jit(solution)/shard_map/squeeze | solution.py:18
  19.5 4.7 %gather_fusion.1 = bf16[512,512]{1,0:T(8,128)(2,1)S(1)} fusion(bf16[4096,512]{1,0:T(8,128)(2,1)} %get-tuple-element.48, s32[1024]{0:T(1024)S(1)} %pad_clamp_fusion), kind=kCustom, calls=%fused_computation.1.clone | custom fusion | bytes 1050624 | tf_op jit(solution)/shard_map/jit(_take)/gather | solution.py:18
  24.3 4.7 %gather_fusion = bf16[512,512]{1,0:T(8,128)(2,1)S(1)} fusion(bf16[4096,512]{1,0:T(8,128)(2,1)} %get-tuple-element.47, s32[1024]{0:T(1024)S(1)} %pad_clamp_fusion.1), kind=kCustom, calls=%fused_computation.clone | custom fusion | bytes 1050624 | tf_op jit(solution)/shard_map/jit(_take)/gather | solution.py:18
  29.0 0.6 select_select_fusion
  29.6 0.0 copy-start.3
  29.6 0.0 copy-start.4
  29.6 0.0 copy-start.2
  29.6 0.0 copy-start.8
  29.6 1.1 pad_maximum_fusion
  30.7 0.0 copy-start.5
  30.7 0.0 reduce-scatter.2.cloned.1.call-update
  30.7 0.0 all-gather.2.cloned.1.call-start
  30.8 0.0 copy-done.3
  31.5 0.0 copy-done.4
  31.5 0.0 copy-done.2
  31.5 0.2 fusion.8
  31.7 0.2 fusion.10
  31.9 25.4 %reduce-scatter.2.cloned.1.call-done = bf16[128,1024]{1,0:T(8,128)(2,1)} async-done(((bf16[512,1024]{1,0:T(8,128)(2,1)}), bf16[128,1024]{1,0:T(8,128)(2,1)}) %reduce-scatter.2.cloned.1.call-update) | async-done | bytes 262160 | tf_op jit(solution)/shard_map/reduce_scatter | solution.py:34
  57.4 0.0 copy-done
  57.4 0.0 copy-done.8
  57.4 0.0 copy-start.1
  57.4 1.4 multiply_convert_fusion.1
  58.8 0.0 copy-done.5
  58.8 1.3 fusion.30
  60.1 0.0 copy-done.1
  60.1 1.2 convert_multiply_fusion
  61.2 0.0 all-gather.2.cloned.1.call-update
  61.3 0.0 all-reduce.11.cloned.1.call-start
  61.3 0.4 convolution_bitcast_fusion
  61.7 0.4 convolution_bitcast_fusion.1
  62.1 0.8 pad_maximum_fusion.2
  62.9 1.9 fusion.14
  64.8 0.0 all-reduce.11.cloned.1.call-update
  64.8 13.3 %all-gather.2.cloned.1.call-done = bf16[512,1024]{1,0:T(8,128)(2,1)} async-done(((bf16[128,1024]{1,0:T(8,128)(2,1)}), bf16[512,1024]{1,0:T(8,128)(2,1)}) %all-gather.2.cloned.1.call-update) | async-done | bytes 1048592 | tf_op jit(solution)/shard_map/all_gather | solution.py:78
  78.1 1.8 reshape.29
  80.0 3.8 %copy.25 = bf16[512,2,512]{0,1,2:T(2,128)(2,1)} copy(bf16[512,2,512]{2,1,0:T(2,128)(2,1)S(1)} %reshape.29) | data formatting | bytes 2097152 | tf_op jit(solution)/shard_map/reshape | solution.py:79
  83.8 5.6 %all-to-all-start = ((bf16[512,2,512]{0,1,2:T(2,128)(2,1)}), bf16[512,2,512]{0,1,2:T(2,128)(2,1)S(1)}, u32[]{:S(2)}, u32[]{:S(2)}) async-start(bf16[512,2,512]{0,1,2:T(2,128)(2,1)} %copy.25), calls=%async_computation.1 | async-start | bytes 2097152 | tf_op jit(solution)/shard_map/all_to_all | solution.py:81
  89.4 0.0 all-reduce.9.cloned.1.call-start
  89.4 46.2 %all_gather.10 = s32[4096,2]{0,1:T(2,128)S(1)} all-gather(s32[512,2]{0,1:T(2,128)S(1)} %get-tuple-element.55), channel_id=1, replica_groups=mesh['dp'=8,'grp'=4] {'dp'}, dimensions={0}, use_global_device_ids=true | all-gather | bytes 36864 | tf_op jit(solution)/shard_map/all_gather | solution.py:82
  135.7 5.4 %all-reduce.11.cloned.1.call-done = (f32[2,128,512]{2,1,0:T(8,128)}, f32[1024,512]{1,0:T(8,128)}) async-done(((f32[2,128,512]{2,1,0:T(8,128)}, f32[1024,512]{1,0:T(8,128)}), (f32[2,128,512]{2,1,0:T(8,128)}, f32[1024,512]{1,0:T(8,128)})) %all-reduce.11.cloned.1.call-update) | async-done | bytes 2621456 | tf_op jit(solution)/shard_map/psum | solution.py:76
  141.1 0.0 all-reduce.9.cloned.1.call-update
  141.2 0.0 copy-done.6
  141.2 0.1 fusion.19
  141.3 0.0 copy-done.7
  141.3 0.2 and_reduce_fusion
  141.5 0.1 fusion.29
  141.7 0.2 fusion.25
  141.8 6.5 %all-reduce.4 = (f32[512]{0:T(512)S(1)}, f32[512]{0:T(512)S(1)}, f32[1]{0:T(128)}) all-reduce(f32[512]{0:T(512)S(1)} %fusion.29, f32[512]{0:T(512)S(1)} %bitcast.59, f32[1]{0:T(128)} %bitcast.19), channel_id=1, replica_groups=mesh['dp'=8,'grp'=4] {'grp'}, use_global_device_ids=true, to_apply=%region_8.10 | all-reduce | flops 1025 | bytes 8200 | tf_op jit(solution)/shard_map/psum | solution.py:76
  148.4 23.9 %all-reduce.2 = (f32[512]{0:T(512)}, f32[512]{0:T(512)}, f32[1]{0:T(128)}) all-reduce(f32[512]{0:T(512)S(1)} %get-tuple-element.40, f32[512]{0:T(512)S(1)} %get-tuple-element.41, f32[1]{0:T(128)} %get-tuple-element.42), channel_id=1, replica_groups=mesh['dp'=8,'grp'=4] {'dp'}, use_global_device_ids=true, to_apply=%region_9.11 | all-reduce | flops 1025 | bytes 8200 | tf_op jit(solution)/shard_map/psum | solution.py:75
  172.3 0.0 all-to-all-done
  172.3 0.2 copy.26
  172.5 0.1 copy.34
  172.6 1.2 fusion.4
  173.8 1.9 copy.28
  175.7 1.8 copy.29
  177.5 24.8 %scatter_custom_fusion = f32[8192,64]{1,0:T(8,128)} fusion(s32[4096]{0:T(1024)S(1)} %get-tuple-element.67, f32[4096,64]{1,0:T(8,128)} %copy.28, f32[]{:T(128)} %constant.3.clone.1), kind=kCustom, calls=%fused_computation.6 | custom fusion | flops 262144 | bytes 2097664
  202.3 24.2 %scatter_fusion = f32[8192,64]{1,0:T(8,128)} fusion(f32[8192,64]{1,0:T(8,128)} %scatter_custom_fusion, s32[4096]{0:T(1024)S(1)} %get-tuple-element.66, f32[4096,64]{1,0:T(8,128)S(1)} %copy.29), kind=kCustom, calls=%fused_computation.3 | custom fusion | flops 262144 | bytes 3162112
  226.6 3.9 %copy.31 = f32[2,4096,64]{1,2,0:T(8,128)} copy(f32[2,4096,64]{2,1,0:T(8,128)} %bitcast.52) | data formatting | bytes 4194304
  230.4 31.1 %all-reduce.9.cloned.1.call-done = (f32[2,128,512]{2,1,0:T(8,128)}, f32[1024,512]{1,0:T(8,128)}) async-done(((f32[2,128,512]{2,1,0:T(8,128)}, f32[1024,512]{1,0:T(8,128)}), (f32[2,128,512]{2,1,0:T(8,128)}, f32[1024,512]{1,0:T(8,128)})) %all-reduce.9.cloned.1.call-update) | async-done | bytes 2621456 | tf_op jit(solution)/shard_map/psum | solution.py:75
  261.5 1.9 copy.41
  263.3 3.1 %copy.42 = f32[1024,512]{1,0:T(8,128)} copy(f32[1024,512]{1,0:T(8,128)} %get-tuple-element.71) | data formatting | bytes 4194304
  (17 shorter events, 0.2 us)
Async XLA Ops:
  7.2 50.2 %copy-start = (bf16[1024,512]{1,0:T(8,128)(2,1)S(1)}, bf16[1024,512]{1,0:T(8,128)(2,1)}, u32[]{:S(2)}) copy-start(bf16[1024,512]{1,0:T(8,128)(2,1)} %param.16) | copy-start | bytes 3145732
  7.2 50.2 %reduce-scatter.2.cloned.1.call-start = ((), (), s32[]{:S(2)}) async-start(), calls=%async_computation.2 | async-start | bytes 1310720 | tf_op jit(solution)/shard_map/reduce_scatter | solution.py:34
  29.6 1.2 copy-start.3
  29.6 1.9 copy-start.4
  29.6 1.9 copy-start.2
  29.6 27.8 %copy-start.8 = (f32[512]{0:T(512)S(1)}, f32[512]{0:T(512)}, u32[]{:S(2)}) copy-start(f32[512]{0:T(512)} %param.17) | copy-start | bytes 6148
  30.7 28.1 %copy-start.5 = (s32[128]{0:T(128)S(1)}, s32[128]{0:T(128)}, u32[]{:S(2)}) copy-start(s32[128]{0:T(128)} %param.13) | copy-start | bytes 1540
  30.7 47.4 %all-gather.2.cloned.1.call-start = ((), (), s32[]{:S(2)}) async-start(), calls=%async_computation.3 | async-start | bytes 1310720 | tf_op jit(solution)/shard_map/all_gather | solution.py:78
  57.4 2.7 copy-start.1
  61.3 79.8 %all-reduce.11.cloned.1.call-start = ((), (), s32[]{:S(2)}) async-start(), calls=%async_computation.5 | async-start | bytes 5242880 | tf_op jit(solution)/shard_map/psum | solution.py:76
  83.8 57.4 %copy-start.6 = (s32[2]{0:T(128)S(1)}, s32[2]{0:T(128)}, u32[]{:S(2)}) copy-start(s32[2]{0:T(128)} %constant.13) | copy-start | bytes 28
  83.8 57.6 %copy-start.7 = (s32[2]{0:T(128)S(1)}, s32[2]{0:T(128)}, u32[]{:S(2)}) copy-start(s32[2]{0:T(128)} %constant.28) | copy-start | bytes 28
  83.8 88.6 %all-to-all-start = ((bf16[512,2,512]{0,1,2:T(2,128)(2,1)}), bf16[512,2,512]{0,1,2:T(2,128)(2,1)S(1)}, u32[]{:S(2)}, u32[]{:S(2)}) async-start(bf16[512,2,512]{0,1,2:T(2,128)(2,1)} %copy.25), calls=%async_computation.1 | async-start | bytes 2097152 | tf_op jit(solution)/shard_map/all_to_all | solution.py:81
  89.4 172.1 %all-reduce.9.cloned.1.call-start = ((), (), s32[]{:S(2)}) async-start(), calls=%async_computation.4 | async-start | bytes 5242880 | tf_op jit(solution)/shard_map/psum | solution.py:75
Sparse Core Ops, SparseCore 0:
  30.8 26.4 reduce-scatter.1
  61.4 16.6 all-gather.1
  81.1 59.9 all-reduce.10
  144.7 116.6 all-reduce.8
